TPU v7x, 256 devices: a whole 4x4x8 slice. The times are simulated.
256 devices in a mesh: vox: 128 (over x, z, y), sub: 2 (over core).
Axes of the slice: x: 4, y: 4, z: 8, core: 2. Of those that a mesh axis runs over, the one named last changes fastest.
Arguments:
- movie: bfloat16 [262144, 4096], P(('vox', 'sub')), may hold values from -120 to 120
- test_matrix: bfloat16 [4096, 256], replicated, may hold values from -0.09375 to 0.09375
Outputs:
- basis: float32 [262144, 256], P(('vox', 'sub'))
- r_factor: float32 [256, 256], replicated
- projected: float32 [256, 4096], P(None, ('vox', 'sub'))
All inputs are finite; a program needn't handle non-finite values.
Results may differ from a plain program's by a relative error of at most 0.00063.
Values sent between devices are 32-bit elements; how exact they have to be, the bound alone decides.
A program may use at most 128 MiB of HBM per device.

v0:
```python
import jax
import jax.numpy as jnp
from jax import lax
from jax.sharding import PartitionSpec as P


def square_sum(matrix):
    return jnp.dot(matrix.T, matrix, precision=lax.Precision.HIGHEST)


def local(movie, test_matrix):
    sketch = jnp.dot(movie, test_matrix, preferred_element_type=jnp.float32)
    devices_all = lax.axis_size(("vox", "sub"))
    sketch_b = sketch.astype(jnp.bfloat16)
    partial_sum = lax.dot_general(
        sketch_b, movie, (((0,), (0,)), ((), ())), preferred_element_type=jnp.float32
    )
    columns = movie.shape[1] // devices_all
    total = lax.psum(partial_sum, ("vox", "sub"))
    mine = lax.dynamic_slice_in_dim(total, lax.axis_index(("vox", "sub")) * columns, columns, 1)
    gram = lax.psum(square_sum(sketch), ("vox", "sub"))
    lower = jnp.linalg.cholesky(gram)
    width = sketch.shape[1]
    identity = jnp.eye(width, dtype=jnp.float32)
    inverse = lax.linalg.triangular_solve(lower, identity, left_side=True, lower=True)
    scale = jnp.sqrt(jnp.float32(sketch.shape[0] * devices_all))
    basis = jnp.dot(sketch, inverse.T, precision=lax.Precision.HIGHEST) * scale
    projected = jnp.dot(inverse, mine, precision=lax.Precision.HIGHEST)
    return (basis, lower.T / scale, projected)


def solution(mesh):
    placed = (P(("vox", "sub"), None), P())
    return jax.shard_map(
        local,
        mesh=mesh,
        in_specs=placed,
        out_specs=(P(("vox", "sub"), None), P(), P(None, ("vox", "sub"))),
        check_vma=False,
    )
```

profile of v0, /device:TPU:2, one launch (start us, length us, event | category | flops | bytes accessed | tf_op | source)
XLA Modules:
  0.0 380.6 jit_solution(14960276804258986143)
XLA Ops:
  7.2 0.0 all-reduce.4.cloned.1.call-start
  7.2 1.5 copy-done
  8.8 5.9 %fusion.17 = f32[1024,256]{1,0:T(8,128)S(1)} fusion(bf16[1024,4096]{1,0:T(8,128)(2,1)} %param.2, bf16[4096,256]{1,0:T(8,128)(2,1)S(1)} %copy-done), kind=kOutput, calls=%fused_computation.40 | convolution fusion | flops 2147483648 | bytes 11534336 | tf_op jit(solution)/shard_map/dot_general | solution.py:12
  14.6 4.3 %fusion = f32[256,4096]{1,0:T(8,128)} fusion(bf16[1024,4096]{1,0:T(8,128)(2,1)S(1)} %copy-done.1, f32[1024,256]{1,0:T(8,128)S(1)} %fusion.17), kind=kOutput, calls=%fused_computation.5 | convolution fusion | flops 2147745792 | bytes 13631488 | tf_op jit(solution)/shard_map/dot_general | solution.py:15
  19.0 2.5 fusion.18
  21.5 0.0 all-reduce.4.cloned.1.call-update
  21.6 0.6 iota_compare_fusion
  22.2 274.1 %all-reduce.4.cloned.1.call-done = (f32[256,256]{0,1:T(8,128)}, f32[256,4096]{1,0:T(8,128)}) async-done(((f32[256,256]{0,1:T(8,128)}, f32[256,4096]{1,0:T(8,128)}), (f32[256,256]{0,1:T(8,128)}, f32[256,4096]{1,0:T(8,128)})) %all-reduce.4.cloned.1.call-update) | async-done | bytes 4456464 | tf_op jit(solution)/shard_map/psum | solution.py:21
  296.3 1.1 copy.6
  297.3 1.0 fusion.2
  298.3 0.7 copy-done.3
  299.0 11.7 %cholesky.50 = f32[128,128]{1,0:T(8,128)S(1)} custom-call(f32[128,128]{1,0:T(8,128)S(1)} %cholesky.118), custom_call_target="Cholesky" | custom-call | tf_op jit(solution)/shard_map/jit(cholesky)/cholesky | solution.py:22
  310.8 9.8 %custom-call.14 = f32[1,128,128]{1,2,0:T(8,128)S(1)} custom-call(f32[1,128,128]{2,1,0:T(8,128)S(1)} %get-tuple-element.31), custom_call_target="InvertDiagBlocksLowerTriangular" | custom-call | tf_op jit(solution)/shard_map/jit(cholesky)/cholesky | solution.py:22
  320.6 0.2 cholesky.113
  320.8 1.0 constant_dynamic-update-slice_fusion
  321.9 1.1 convolution_subtract_fusion.1
  323.0 11.7 %cholesky.105 = f32[128,128]{1,0:T(8,128)S(1)} custom-call(f32[128,128]{1,0:T(8,128)S(1)} %convolution_subtract_fusion.1), custom_call_target="Cholesky" | custom-call | tf_op jit(solution)/shard_map/jit(cholesky)/cholesky | solution.py:22
  334.7 0.7 compare_reduce_fusion
  336.7 1.7 multiply_bitcast_fusion
  338.4 0.1 triangular_solve.63
  338.5 5.2 %while.1 = (s32[]{:T(128)}, f32[256,256]{1,0:T(8,128)S(1)}, s32[2,2]{1,0:T(2,128)S(1)}, f32[2,128,128]{2,1,0:T(8,128)}, s32[]{:T(128)}) while((s32[]{:T(128)}, f32[256,256]{1,0:T(8,128)S(1)}, s32[2,2]{1,0:T(2,128)S(1)}, f32[2,128,128]{2,1,0:T(8,128)}, s32[]{:T(128)}) %tuple.29), condition=%wide.while_cond, body=%wide.while_body.sunk | while | flops 2 | bytes 132705 | solution.py:25
  338.5 0.6 fusion.30
  339.1 2.0 bitcast_dynamic-update-slice_fusion.2
  341.1 0.6 fusion.30
  341.7 2.0 bitcast_dynamic-update-slice_fusion.2
  343.7 21.1 %custom-call.15 = f32[2,128,128]{1,2,0:T(8,128)} custom-call(f32[2,128,128]{2,1,0:T(8,128)} %get-tuple-element.10), custom_call_target="InvertDiagBlocksLowerTriangular" | custom-call | tf_op jit(solution)/shard_map/triangular_solve | solution.py:25
  364.8 1.1 fusion.6
  365.9 1.0 convolution_subtract_fusion
  366.9 1.2 fusion.9
  368.1 2.0 convolution_multiply_fusion
  370.1 1.8 copy.7
  371.8 1.9 fusion.4
  (13 shorter events, 0.1 us)
Async XLA Ops:
  7.2 1.6 copy-start
  7.2 289.1 %all-reduce.4.cloned.1.call-start = ((), (), s32[]{:S(2)}) async-start(), calls=%async_computation | async-start | bytes 8912896 | tf_op jit(solution)/shard_map/psum | solution.py:21
  8.8 5.9 %copy-start.1 = (bf16[1024,4096]{1,0:T(8,128)(2,1)S(1)}, bf16[1024,4096]{1,0:T(8,128)(2,1)}, u32[]{:S(2)}) copy-start(bf16[1024,4096]{1,0:T(8,128)(2,1)} %param.2) | copy-start | bytes 25165828
  298.3 0.7 copy-start.3
  334.7 2.0 copy-start.2
Sparse Core Ops, SparseCore 0:
  21.7 274.5 all-reduce.3
where the time goes:
time: 381 us
  waiting for transfers between devices  274 us (72%)
  other arithmetic  58.5 us (15%)
  matrix products  22.1 us (6%)
  between operations  15.4 us (4%)
  local copies, waits for them, and re-layouts  10.6 us (3%)
    psum x1, waiting for transfers between devices, local(): gram = lax.psum(square_sum(sketch), ('vox', 'sub'))  274 us
    another operation x6, other arithmetic, local(): lower = jnp.linalg.cholesky(gram)  34 us
    another operation x2, other arithmetic, local(): lax.linalg.triangular_solve(lower, identity, left_side=True, lower=True)  21.1 us
  transfers between devices with their start and end apart: 1, of which 1 were waited for; matrix products, arithmetic and copies ran while one was open for 0% of the time, Pallas kernels for 0%

commit v1 on v0

--- a/solution.py
+++ b/solution.py
@@ -18,7 +18,10 @@
     columns = movie.shape[1] // devices_all
     total = lax.psum(partial_sum, ("vox", "sub"))
     mine = lax.dynamic_slice_in_dim(total, lax.axis_index(("vox", "sub")) * columns, columns, 1)
-    gram = lax.psum(square_sum(sketch), ("vox", "sub"))
+    try_all_the_scenes = lambda tile_in, mesh_dim, dev_axis: lax.psum(
+        lax.psum(tile_in, axis_name=mesh_dim), axis_name=dev_axis
+    )
+    gram = try_all_the_scenes(square_sum(sketch), "vox", "sub")
     lower = jnp.linalg.cholesky(gram)
     width = sketch.shape[1]
     identity = jnp.eye(width, dtype=jnp.float32)

time: 381 us -> 552 us (1.45)
  waiting for transfers between devices: 274 us -> 442 us
    psum x1 -> x3, waiting for transfers between devices: 274 us -> 442 us  [the longest x1 219 us: local(): lax.psum(tile_in, axis_name=mesh_dim)]
  transfers between devices with their start and end apart: 1 -> 3, of which waited for: 1 -> 3; matrix products, arithmetic and copies ran while one was open for 0% -> 15% of each run, Pallas kernels for 0% -> 0%
where the time goes in v1:
time: 552 us; the launch traced here: 551 us
  waiting for transfers between devices  442 us (80%)
  other arithmetic  58.5 us (11%)
  matrix products  25.3 us (5%)
  between operations  15.1 us (3%)
  local copies, waits for them, and re-layouts  10.2 us (2%)
    psum x1, waiting for transfers between devices, local(): lax.psum(tile_in, axis_name=mesh_dim)  219 us
    psum x1, waiting for transfers between devices, local(): total = lax.psum(partial_sum, ('vox', 'sub'))  202 us
    another operation x6, other arithmetic, local(): lower = jnp.linalg.cholesky(gram)  34.1 us
    another operation x2, other arithmetic, local(): lax.linalg.triangular_solve(lower, identity, left_side=True, lower=True)  21.1 us
    psum x1, waiting for transfers between devices, local(): lax.psum(lax.psum(tile_in, axis_name=mesh_dim), axis_name=dev_axis)  20.6 us
  transfers between devices with their start and end apart: 3, of which 3 were waited for; matrix products, arithmetic and copies ran while one was open for 15% of the time, Pallas kernels for 0%

profile of v1, /device:TPU:2, one launch (start us, length us, event | category | flops | bytes accessed | tf_op | source)
XLA Modules:
  0.0 551.1 jit_solution(4584890378576869725)
XLA Ops:
  7.2 1.5 copy-done
  8.8 5.7 %fusion.17 = f32[1024,256]{1,0:T(8,128)S(1)} fusion(bf16[1024,4096]{1,0:T(8,128)(2,1)} %param.2, bf16[4096,256]{1,0:T(8,128)(2,1)S(1)} %copy-done), kind=kOutput, calls=%fused_computation.40 | convolution fusion | flops 2147483648 | bytes 11534336 | tf_op jit(solution)/shard_map/dot_general | solution.py:12
  14.5 2.5 fusion.18
  17.1 218.7 %all-reduce.5.cloned.1.call-done = f32[256,256]{0,1:T(8,128)} async-done(((f32[256,256]{0,1:T(8,128)}), f32[256,256]{0,1:T(8,128)}) %all-reduce.5.cloned.1.call-update) | async-done | bytes 262160 | tf_op jit(solution)/shard_map/psum | solution.py:22
  235.8 0.2 all-reduce.9.cloned.1.call-start
  236.1 7.7 %fusion = f32[256,4096]{1,0:T(8,128)} fusion(bf16[1024,4096]{1,0:T(8,128)(2,1)} %param.2, f32[1024,256]{1,0:T(8,128)S(1)} %fusion.17), kind=kOutput, calls=%fused_computation.5 | convolution fusion | flops 2147745792 | bytes 13631488 | tf_op jit(solution)/shard_map/dot_general | solution.py:15
  243.8 0.6 iota_compare_fusion
  244.5 20.6 %all-reduce.7.cloned.1.call-done = f32[256,256]{0,1:T(8,128)} async-done(((f32[256,256]{0,1:T(8,128)}), f32[256,256]{0,1:T(8,128)}) %all-reduce.7.cloned.1.call-update) | async-done | bytes 262160 | tf_op jit(solution)/shard_map/psum | solution.py:21
  265.0 1.1 copy.6
  266.1 1.0 fusion.2
  267.1 0.7 copy-done.2
  267.8 11.7 %cholesky.50 = f32[128,128]{1,0:T(8,128)S(1)} custom-call(f32[128,128]{1,0:T(8,128)S(1)} %cholesky.118), custom_call_target="Cholesky" | custom-call | tf_op jit(solution)/shard_map/jit(cholesky)/cholesky | solution.py:25
  279.6 9.8 %custom-call.14 = f32[1,128,128]{1,2,0:T(8,128)S(1)} custom-call(f32[1,128,128]{2,1,0:T(8,128)S(1)} %get-tuple-element.29), custom_call_target="InvertDiagBlocksLowerTriangular" | custom-call | tf_op jit(solution)/shard_map/jit(cholesky)/cholesky | solution.py:25
  289.4 1.0 constant_dynamic-update-slice_fusion
  290.5 1.1 convolution_subtract_fusion.1
  291.6 11.9 %cholesky.105 = f32[128,128]{1,0:T(8,128)S(1)} custom-call(f32[128,128]{1,0:T(8,128)S(1)} %convolution_subtract_fusion.1), custom_call_target="Cholesky" | custom-call | tf_op jit(solution)/shard_map/jit(cholesky)/cholesky | solution.py:25
  303.5 0.6 compare_reduce_fusion
  305.3 1.7 multiply_bitcast_fusion
  307.0 0.1 triangular_solve.63
  307.1 5.0 while.1
  307.1 0.6 fusion.30
  307.7 1.9 bitcast_dynamic-update-slice_fusion.2
  309.6 0.6 fusion.30
  310.2 1.9 bitcast_dynamic-update-slice_fusion.2
  312.1 21.1 %custom-call.15 = f32[2,128,128]{1,2,0:T(8,128)} custom-call(f32[2,128,128]{2,1,0:T(8,128)} %get-tuple-element.10), custom_call_target="InvertDiagBlocksLowerTriangular" | custom-call | tf_op jit(solution)/shard_map/triangular_solve | solution.py:28
  333.2 1.8 copy.7
  335.0 1.1 fusion.6
  336.1 1.0 convolution_subtract_fusion
  337.2 1.1 fusion.9
  338.3 2.0 convolution_multiply_fusion
  340.3 202.3 %all-reduce.9.cloned.1.call-done = f32[256,4096]{1,0:T(8,128)} async-done(((f32[256,4096]{1,0:T(8,128)}), f32[256,4096]{1,0:T(8,128)}) %all-reduce.9.cloned.1.call-update) | async-done | bytes 4194320 | tf_op jit(solution)/shard_map/psum | solution.py:19
  542.6 1.9 fusion.4
  (17 shorter events, 0.3 us)
Async XLA Ops:
  7.2 1.6 copy-start
  7.2 228.6 %all-reduce.5.cloned.1.call-start = ((), (), s32[]{:S(2)}) async-start(), calls=%async_computation | async-start | bytes 524288 | tf_op jit(solution)/shard_map/psum | solution.py:22
  17.0 248.0 %all-reduce.7.cloned.1.call-start = ((), (), s32[]{:S(2)}) async-start(), calls=%async_computation.1 | async-start | bytes 524288 | tf_op jit(solution)/shard_map/psum | solution.py:21
  235.8 306.7 %all-reduce.9.cloned.1.call-start = ((), (), s32[]{:S(2)}) async-start(), calls=%async_computation.2 | async-start | bytes 8388608 | tf_op jit(solution)/shard_map/psum | solution.py:19
  267.1 0.7 copy-start.2
  303.5 1.9 copy-start.1
Sparse Core Ops, SparseCore 0:
  17.1 218.6 all-reduce.4
  238.4 26.5 all-reduce.6
  270.5 272.0 all-reduce.8
